TPU v7x, 512 devices: a 4x2x32 block of a 4x8x32 slice. The times are simulated.
512 devices in a mesh: groups: 2 (over y), ctx: 32 (over z), rep: 4 (over x), row: 2 (over core).
Axes of the slice: x: 4, y: 2, z: 32, core: 2. Of those that a mesh axis runs over, the one named last changes fastest.
The devices are a block of a 4x8x32 slice.
Arguments:
- queries: bfloat16 [4, 128, 64, 128], P(None, ('groups', 'ctx', 'row'), 'rep'), parts along dimension 1, may hold values from -8 to 8
- new_keys: bfloat16 [4, 128, 8, 128], P(None, ('groups', 'ctx', 'row'), 'rep'), parts along dimension 1, may hold values from -4.5 to 4.5
- step_new_values: bfloat16 [4, 128, 8, 128], P(None, ('groups', 'ctx', 'row'), 'rep'), parts along dimension 1, may hold values from -6 to 6
- context_keys: bfloat16 [8, 32768, 128], P('rep', ('groups', 'ctx')), parts along dimension 1, may hold values from -6 to 6
- context_values: bfloat16 [8, 32768, 128], P('rep', ('groups', 'ctx')), parts along dimension 1, may hold values from -6 to 6
- cluster_centroid_keys: bfloat16 [8, 256, 128], P('rep', ('groups', 'ctx')), parts along dimension 1, may hold values from -4 to 4
- cluster_mean_values: bfloat16 [8, 256, 128], P('rep', ('groups', 'ctx')), parts along dimension 1, may hold values from -6 to 6
- cluster_page_slot: int32 [8, 256], P('rep', 'groups'), parts along dimension 1, may hold values from 0 to 127, each once within a row
- picks: int32 [128, 8, 16], P(('groups', 'ctx', 'row'), 'rep'), parts along dimension 0, may hold values from 0 to 127, all different within a row
Outputs:
- attention: bfloat16 [4, 128, 64, 128], P(None, ('groups', 'ctx', 'row'), 'rep'), parts along dimension 1
There are 2 independent parts, one for each index of `groups`. A program takes and returns all parts, laid end to end along the dimension named above; each array names one. Nothing has to cross between parts.
Inputs may be any that keep to these rules, and one draw needn't show every extreme that they name: `picks`: for each row and key-value head, 16 different cluster ids. `cluster_page_slot`: for each key-value head, every cluster has its own page slot; slot p lies on context shard p // 4.
All inputs are finite; a program needn't handle non-finite values.
Results may differ from a plain program's by a relative error of at most 0.0027.
Values may be sent and summed in bfloat16 or wider, within the bound.
No kernel may reach another device: no remote copies, remote signals or barrier semaphores. Data moves between devices by JAX's collectives and lax.ppermute only.
A program may use at most 64 MiB of HBM per device.

v0:
```python
import math
import jax
import jax.numpy as jnp
from jax import lax
from jax.sharding import PartitionSpec as P

FLOOR_SCORE = -10000.0


def from_everyone(x, axis):
    peers = lax.axis_size(axis)
    return lax.all_to_all(jnp.broadcast_to(x[None], (peers, *x.shape)), axis, 0, 0, tiled=True)


def laid_out(pieces, dim):
    lengths = list(pieces.shape[1:])
    lengths[dim] *= pieces.shape[0]
    return jnp.moveaxis(pieces, 0, dim).reshape(lengths)


def gather_directly(x, axis, dim):
    pieces = from_everyone(x, axis)
    return laid_out(pieces, dim)


def tail_block(queries, new_keys, step_new_values, logit_multiplier):
    num_steps, num_rows, num_heads, head_width = queries.shape
    kv_heads = new_keys.shape[2]
    grouped = queries.astype(jnp.float32).reshape(
        num_steps, num_rows, kv_heads, num_heads // kv_heads, head_width
    )
    scores = (
        jnp.einsum("srhgd,trhd->srhgt", grouped, new_keys.astype(jnp.float32)) * logit_multiplier
    )
    step_ids = jnp.arange(num_steps, dtype=jnp.int32)
    causal = (step_ids[None, :] <= step_ids[:, None])[:, None, None, None, :]
    block_top = jnp.max(jnp.where(causal, scores, FLOOR_SCORE), axis=-1)
    weights = jnp.where(causal, jnp.exp(scores - block_top[..., None]), 0.0)
    sum_total = jnp.sum(weights, axis=-1)
    rounded = weights.astype(jnp.bfloat16).astype(jnp.float32)
    tail_out = jnp.einsum("srhgt,trhd->srhgd", rounded, step_new_values.astype(jnp.float32))
    return (
        tail_out.reshape(num_steps, num_rows, num_heads, head_width),
        sum_total.reshape(num_steps, num_rows, num_heads),
        block_top.reshape(num_steps, num_rows, num_heads),
    )


def per_device(
    queries,
    new_keys,
    step_new_values,
    context_keys,
    context_values,
    cluster_centroid_keys,
    cluster_mean_values,
    cluster_page_slot,
    picks,
):
    num_steps = queries.shape[0]
    num_heads = queries.shape[2]
    head_width = queries.shape[3]
    kv_local = context_keys.shape[0]
    span_tokens = context_keys.shape[1]
    cl_local = cluster_centroid_keys.shape[1]
    grouping_member_entries = span_tokens // cl_local
    query_group_size = num_heads // kv_local
    logit_multiplier = 1.0 / math.sqrt(head_width)
    membership_log_weight = math.log(grouping_member_entries)
    shard_index = lax.axis_index("ctx")
    gathered = lax.all_gather(queries, "ctx", axis=1, tiled=True)
    chosen = gather_directly(picks, "ctx", 0)
    rows_all = gathered.shape[1]
    cluster_ids = jnp.arange(cluster_page_slot.shape[1], dtype=jnp.int32)
    pick_hits = chosen[..., None] == cluster_ids
    picked_slots = jnp.sum(jnp.where(pick_hits, cluster_page_slot[None, :, None, :], 0), axis=-1)
    local_ids = shard_index * cl_local + jnp.arange(cl_local, dtype=jnp.int32)
    slot_used = jnp.any(picked_slots[..., None] == local_ids, axis=2)
    cluster_used = jnp.any(chosen[..., None] == local_ids, axis=2)
    step_outs, step_totals, step_tops = ([], [], [])
    for step_index in range(num_steps):
        head_outs, head_totals, head_tops = ([], [], [])
        for current_head_index in range(kv_local):
            generation_probe_vectors = gathered[
                step_index,
                :,
                current_head_index * query_group_size : (current_head_index + 1) * query_group_size,
                :,
            ].reshape(rows_all * query_group_size, head_width)
            exact_mask = slot_used[:, current_head_index][:, None, :, None]
            coarse_mask = jnp.logical_not(cluster_used[:, current_head_index])[:, None, :]
            exact_scores = (
                jnp.einsum(
                    "qd,kd->qk",
                    generation_probe_vectors,
                    context_keys[current_head_index],
                    preferred_element_type=jnp.float32,
                )
                * logit_multiplier
            )
            exact_scores = exact_scores.reshape(
                rows_all, query_group_size, cl_local, grouping_member_entries
            )
            prototype_logits = (
                jnp.einsum(
                    "qd,kd->qk",
                    generation_probe_vectors,
                    cluster_centroid_keys[current_head_index],
                    preferred_element_type=jnp.float32,
                )
                * logit_multiplier
                + membership_log_weight
            )
            prototype_logits = prototype_logits.reshape(rows_all, query_group_size, cl_local)
            block_top = jnp.maximum(
                jnp.max(jnp.where(exact_mask, exact_scores, FLOOR_SCORE), axis=(2, 3)),
                jnp.max(jnp.where(coarse_mask, prototype_logits, FLOOR_SCORE), axis=2),
            )
            exact_weights = jnp.where(
                exact_mask, jnp.exp(exact_scores - block_top[:, :, None, None]), 0.0
            )
            coarse_weights = jnp.where(
                coarse_mask, jnp.exp(prototype_logits - block_top[:, :, None]), 0.0
            )
            sum_total = jnp.sum(exact_weights, axis=(2, 3)) + jnp.sum(coarse_weights, axis=2)
            block_out = jnp.dot(
                exact_weights.astype(jnp.bfloat16).reshape(
                    rows_all * query_group_size, span_tokens
                ),
                context_values[current_head_index],
                preferred_element_type=jnp.float32,
            )
            block_out = block_out + jnp.dot(
                coarse_weights.astype(jnp.bfloat16).reshape(rows_all * query_group_size, cl_local),
                cluster_mean_values[current_head_index],
                preferred_element_type=jnp.float32,
            )
            head_outs.append(block_out.reshape(rows_all, query_group_size, head_width))
            head_totals.append(sum_total)
            head_tops.append(block_top)
        step_outs.append(jnp.concatenate(head_outs, axis=1))
        step_totals.append(jnp.concatenate(head_totals, axis=1))
        step_tops.append(jnp.concatenate(head_tops, axis=1))
    partial_outs = jnp.stack(step_outs)
    partial_totals = jnp.stack(step_totals)
    partial_tops = jnp.stack(step_tops)
    got_tops, got_totals, got_outs = (
        lax.all_to_all(partial_tops[None], "ctx", split_axis=2, concat_axis=0, tiled=True),
        lax.all_to_all(partial_totals[None], "ctx", split_axis=2, concat_axis=0, tiled=True),
        lax.all_to_all(partial_outs[None], "ctx", split_axis=2, concat_axis=0, tiled=True),
    )
    best_top = jnp.max(got_tops, axis=0)
    factor = jnp.exp(got_tops - best_top)
    sum_total = jnp.sum(factor * got_totals, axis=0)
    merged = jnp.sum(factor[..., None] * got_outs, axis=0)
    tail_out, tail_total, tail_top = tail_block(
        queries, new_keys, step_new_values, logit_multiplier
    )
    overall = jnp.maximum(best_top, tail_top)
    context_factor = jnp.exp(best_top - overall)
    tail_factor = jnp.exp(tail_top - overall)
    numer = context_factor[..., None] * merged + tail_factor[..., None] * tail_out
    denom = context_factor * sum_total + tail_factor * tail_total
    return (numer / denom[..., None]).astype(jnp.bfloat16)


def solution(mesh):
    return jax.shard_map(
        per_device,
        mesh=mesh,
        in_specs=(
            P(None, ("groups", "ctx", "row"), "rep", None),
            P(None, ("groups", "ctx", "row"), "rep", None),
            P(None, ("groups", "ctx", "row"), "rep", None),
            P("rep", ("groups", "ctx"), None),
            P("rep", ("groups", "ctx"), None),
            P("rep", ("groups", "ctx"), None),
            P("rep", ("groups", "ctx"), None),
            P("rep", "groups"),
            P(("groups", "ctx", "row"), "rep", None),
        ),
        out_specs=P(None, ("groups", "ctx", "row"), "rep", None),
        check_vma=False,
    )
```

profile of v0, /device:TPU:46, one launch (start us, length us, event | category | flops | bytes accessed | tf_op | source)
XLA Modules:
  0.0 299.1 jit_solution(11759617294997700711)
XLA Ops:
  0.0 0.7 copy-done.7
  0.7 0.6 broadcast_in_dim.256
  1.3 45.9 %all-to-all-start = ((s32[32,1,2,16]{3,2,1,0:T(2,128)}), s32[32,1,2,16]{3,2,1,0:T(2,128)S(1)}, u32[]{:S(2)}, u32[]{:S(2)}) async-start(s32[32,1,2,16]{3,2,1,0:T(2,128)} %broadcast_in_dim.256), calls=%async_computation | async-start | bytes 65536 | tf_op jit(solution)/shard_map/all_to_all | solution.py:12
  47.2 59.1 %all_gather.3 = bf16[4,32,16,128]{3,2,1,0:T(8,128)(2,1)S(1)} all-gather(bf16[4,1,16,128]{3,2,1,0:T(8,128)(2,1)S(1)} %copy-done.5), channel_id=1, replica_groups=mesh['groups'=2,'ctx'=32,'rep'=4,'row'=2] {'ctx'}, dimensions={1}, use_global_device_ids=true | all-gather | bytes 540672 | tf_op jit(solution)/shard_map/all_gather | solution.py:71
  106.3 0.1 fusion.9
  106.5 0.1 fusion.10
  106.6 0.1 fusion.11
  106.8 0.2 fusion.12
  106.9 0.1 fusion.13
  107.1 0.2 fusion.14
  107.2 0.2 copy-done.1
  107.4 0.2 convolution_multiply_fusion.2
  107.7 0.2 convolution_multiply_fusion.3
  107.9 0.2 convolution_multiply_fusion.4
  108.2 0.2 convolution_multiply_fusion.5
  108.5 0.6 copy-done.6
  109.1 1.4 select_reduce_fusion
  110.6 0.1 compare_reduce_fusion
  110.7 0.1 copy.51
  110.9 0.1 broadcast_in_dim.272
  111.0 1.2 fusion.22
  112.2 1.0 select_reduce_fusion.8
  113.3 0.4 fusion.48
  113.7 1.4 fusion.34
  115.1 0.4 fusion.44
  115.5 0.4 fusion.42
  115.8 0.7 fusion.36
  116.6 0.4 fusion.46
  117.1 0.1 max.136
  117.2 0.1 copy.49
  117.3 0.1 broadcast_in_dim.264
  117.4 0.1 broadcast_in_dim.265
  117.5 1.2 fusion.18
  118.7 1.0 select_reduce_fusion.9
  119.7 0.4 fusion.56
  120.0 1.4 fusion.26
  121.5 0.4 fusion.52
  121.8 0.4 fusion.50
  122.2 0.7 fusion.28
  122.9 0.4 fusion.54
  123.7 0.6 copy-done.4
  124.3 0.2 fusion.6
  124.6 0.2 fusion.4
  124.8 0.2 fusion
  125.0 0.2 fusion.2
  125.7 0.2 fusion.7
  125.9 0.2 fusion.5
  126.1 0.2 fusion.1
  126.4 0.2 fusion.3
  127.3 0.7 copy.58
  128.0 17.9 %all-to-all-start.3 = ((f32[1,4,32,16]{3,1,0,2:T(4,128)}), f32[1,4,32,16]{3,1,0,2:T(4,128)S(1)}, u32[]{:S(2)}, u32[]{:S(2)}) async-start(f32[1,4,32,16]{3,1,0,2:T(4,128)} %copy.58), calls=%async_computation.3 | async-start | bytes 131072 | tf_op jit(solution)/shard_map/all_to_all | solution.py:149
  146.2 0.7 copy.52
  147.0 22.9 %all-to-all-done.3 = f32[1,4,32,16]{3,1,0,2:T(4,128)S(1)} async-done(((f32[1,4,32,16]{3,1,0,2:T(4,128)}), f32[1,4,32,16]{3,1,0,2:T(4,128)S(1)}, u32[]{:S(2)}, u32[]{:S(2)}) %all-to-all-start.3) | async-done | bytes 8224 | tf_op jit(solution)/shard_map/all_to_all | solution.py:149
  169.8 4.8 %all-to-all-start.1 = ((f32[1,4,32,16]{3,1,0,2:T(4,128)}), f32[1,4,32,16]{3,1,0,2:T(4,128)S(1)}, u32[]{:S(2)}, u32[]{:S(2)}) async-start(f32[1,4,32,16]{3,1,0,2:T(4,128)} %copy.52), calls=%async_computation.1 | async-start | bytes 131072 | tf_op jit(solution)/shard_map/all_to_all | solution.py:148
  174.6 1.1 maximum_bitcast_fusion
  175.7 22.7 %all-to-all-done.1 = f32[1,4,32,16]{3,1,0,2:T(4,128)S(1)} async-done(((f32[1,4,32,16]{3,1,0,2:T(4,128)}), f32[1,4,32,16]{3,1,0,2:T(4,128)S(1)}, u32[]{:S(2)}, u32[]{:S(2)}) %all-to-all-start.1) | async-done | bytes 8224 | tf_op jit(solution)/shard_map/all_to_all | solution.py:148
  198.4 4.8 %all-to-all-start.2 = ((f32[1,4,32,16,128]{4,3,1,0,2:T(8,128)}), f32[1,4,32,16,128]{4,3,1,0,2:T(8,128)S(1)}, u32[]{:S(2)}, u32[]{:S(2)}) async-start(f32[1,4,32,16,128]{4,3,1,0,2:T(8,128)} %maximum_bitcast_fusion), calls=%async_computation.2 | async-start | bytes 2097152 | tf_op jit(solution)/shard_map/all_to_all | solution.py:150
  203.3 0.7 copy-done.9
  203.9 0.2 select_reduce_fusion.1
  204.1 0.1 fusion.122
  204.4 0.3 convolution_bitcast_fusion
  204.8 93.2 %all-to-all-done.2 = f32[1,4,32,16,128]{4,3,1,0,2:T(8,128)S(1)} async-done(((f32[1,4,32,16,128]{4,3,1,0,2:T(8,128)}), f32[1,4,32,16,128]{4,3,1,0,2:T(8,128)S(1)}, u32[]{:S(2)}, u32[]{:S(2)}) %all-to-all-start.2) | async-done | bytes 1048608 | tf_op jit(solution)/shard_map/all_to_all | solution.py:150
  298.0 0.3 fusion.17
  298.4 0.7 fusion.121
  (77 shorter events, 2.7 us)
Async XLA Ops:
  0.0 204.4 %copy-start = (bf16[4,1,2,128]{3,2,1,0:T(2,128)(2,1)S(1)}, bf16[4,1,2,128]{3,2,1,0:T(2,128)(2,1)}, u32[]{:S(2)}) copy-start(bf16[4,1,2,128]{3,2,1,0:T(2,128)(2,1)} %param.11) | copy-start | bytes 6148
  0.0 0.7 copy-start.7
  1.3 45.9 %copy-start.5 = (bf16[4,1,16,128]{3,2,1,0:T(8,128)(2,1)S(1)}, bf16[4,1,16,128]{3,2,1,0:T(8,128)(2,1)}, u32[]{:S(2)}) copy-start(bf16[4,1,16,128]{3,2,1,0:T(8,128)(2,1)} %param.9) | copy-start | bytes 49156
  1.3 107.1 %all-to-all-start = ((s32[32,1,2,16]{3,2,1,0:T(2,128)}), s32[32,1,2,16]{3,2,1,0:T(2,128)S(1)}, u32[]{:S(2)}, u32[]{:S(2)}) async-start(s32[32,1,2,16]{3,2,1,0:T(2,128)} %broadcast_in_dim.256), calls=%async_computation | async-start | bytes 65536 | tf_op jit(solution)/shard_map/all_to_all | solution.py:12
  47.2 59.1 %copy-start.8 = (bf16[2,4,128]{2,1,0:T(4,128)(2,1)S(1)}, bf16[2,4,128]{2,1,0:T(4,128)(2,1)}, u32[]{:S(2)}) copy-start(bf16[2,4,128]{2,1,0:T(4,128)(2,1)} %param.14) | copy-start | bytes 6148
  106.3 1.8 copy-start.3
  106.3 1.1 copy-start.1
  108.4 0.7 copy-start.6
  111.0 2.3 copy-start.2
  123.6 0.7 copy-start.4
  128.0 41.9 %all-to-all-start.3 = ((f32[1,4,32,16]{3,1,0,2:T(4,128)}), f32[1,4,32,16]{3,1,0,2:T(4,128)S(1)}, u32[]{:S(2)}, u32[]{:S(2)}) async-start(f32[1,4,32,16]{3,1,0,2:T(4,128)} %copy.58), calls=%async_computation.3 | async-start | bytes 131072 | tf_op jit(solution)/shard_map/all_to_all | solution.py:149
  169.8 28.5 %all-to-all-start.1 = ((f32[1,4,32,16]{3,1,0,2:T(4,128)}), f32[1,4,32,16]{3,1,0,2:T(4,128)S(1)}, u32[]{:S(2)}, u32[]{:S(2)}) async-start(f32[1,4,32,16]{3,1,0,2:T(4,128)} %copy.52), calls=%async_computation.1 | async-start | bytes 131072 | tf_op jit(solution)/shard_map/all_to_all | solution.py:148
  198.4 99.6 %all-to-all-start.2 = ((f32[1,4,32,16,128]{4,3,1,0,2:T(8,128)}), f32[1,4,32,16,128]{4,3,1,0,2:T(8,128)S(1)}, u32[]{:S(2)}, u32[]{:S(2)}) async-start(f32[1,4,32,16,128]{4,3,1,0,2:T(8,128)} %maximum_bitcast_fusion), calls=%async_computation.2 | async-start | bytes 2097152 | tf_op jit(solution)/shard_map/all_to_all | solution.py:150
  203.2 0.7 copy-start.9
where the time goes:
time: 300 us; the launch traced here: 299 us
  waiting for transfers between devices  139 us (46%)
  starting transfers between devices  73.4 us (24%)
  blocking collectives  59.1 us (20%)
  matrix products  14.1 us (5%)
  local copies, waits for them, and re-layouts  7.04 us (2%)
  other arithmetic  6.17 us (2%)
    all_to_all x1, waiting for transfers between devices, per_device(): lax.all_to_all(partial_outs[None], 'ctx', split_axis=2, concat_axis=0, ti...  93.2 us
    all_gather x1, blocking collectives, per_device(): gathered = lax.all_gather(queries, 'ctx', axis=1, tiled=True)  59.1 us
    all_to_all x1, starting transfers between devices, from_everyone(): lax.all_to_all(jnp.broadcast_to(x[None], (peers, *x.shape)), axis, 0, 0,...  45.9 us
    all_to_all x1, waiting for transfers between devices, per_device(): lax.all_to_all(partial_totals[None], 'ctx', split_axis=2, concat_axis=0,...  22.9 us
    all_to_all x1, waiting for transfers between devices, per_device(): lax.all_to_all(partial_tops[None], 'ctx', split_axis=2, concat_axis=0, ti...  22.7 us
    all_to_all x1, starting transfers between devices, per_device(): lax.all_to_all(partial_totals[None], 'ctx', split_axis=2, concat_axis=0,...  17.9 us
    dot_general x8, matrix products, per_device(): jnp.einsum('qd,kd->qk', generation_probe_vectors, context_keys[current_he...  6.08 us
  transfers between devices with their start and end apart: 4, of which 3 were waited for; matrix products, arithmetic and copies ran while one was open for 2% of the time, Pallas kernels for 0%

commit v1 on v0

--- a/solution.py
+++ b/solution.py
@@ -68,7 +68,11 @@
     logit_multiplier = 1.0 / math.sqrt(head_width)
     membership_log_weight = math.log(grouping_member_entries)
     shard_index = lax.axis_index("ctx")
-    gathered = lax.all_gather(queries, "ctx", axis=1, tiled=True)
+    size = lax.axis_size("ctx")
+    repeats = [size if d == 1 else 1 for d in range(queries.ndim)]
+    gathered = lax.all_to_all(
+        jnp.tile(queries, repeats), "ctx", split_axis=1, concat_axis=1, tiled=True
+    )
     chosen = gather_directly(picks, "ctx", 0)
     rows_all = gathered.shape[1]
     cluster_ids = jnp.arange(cluster_page_slot.shape[1], dtype=jnp.int32)

time: 300 us -> 320 us (1.067)
  the two profiles are of different devices: /device:TPU:46 before, /device:TPU:44 now
where the time goes in v1:
time: 320 us
  waiting for transfers between devices  210 us (66%)
  blocking collectives  68.1 us (21%)
  starting transfers between devices  19.3 us (6%)
  matrix products  9.06 us (3%)
  local copies, waits for them, and re-layouts  6.86 us (2%)
  other arithmetic  6.13 us (2%)
    all_to_all x1, waiting for transfers between devices, per_device(): lax.all_to_all(partial_outs[None], 'ctx', split_axis=2, concat_axis=0, ti...  103 us
    all_to_all x1, blocking collectives, from_everyone(): lax.all_to_all(jnp.broadcast_to(x[None], (peers, *x.shape)), axis, 0, 0,...  68.1 us
    all_to_all x1, waiting for transfers between devices, per_device(): lax.all_to_all(jnp.tile(queries, repeats), 'ctx', split_axis=1, concat_ax...  61.1 us
    all_to_all x1, waiting for transfers between devices, per_device(): lax.all_to_all(partial_tops[None], 'ctx', split_axis=2, concat_axis=0, ti...  22.7 us
    all_to_all x1, waiting for transfers between devices, per_device(): lax.all_to_all(partial_totals[None], 'ctx', split_axis=2, concat_axis=0,...  22.7 us
  transfers between devices with their start and end apart: 4, of which 4 were waited for; matrix products, arithmetic and copies ran while one was open for 2% of the time, Pallas kernels for 0%

profile of v1, /device:TPU:44, one launch (start us, length us, event | category | flops | bytes accessed | tf_op | source)
XLA Modules:
  0.0 319.7 jit_solution(12295869245952611823)
XLA Ops:
  0.0 0.7 copy-done.6
  0.7 68.1 %all_to_all.67 = s32[32,1,2,16]{3,2,1,0:T(2,128)S(1)} all-to-all(s32[32,1,2,16]{3,2,1,0:T(2,128)S(1)} %broadcast_in_dim.256), channel_id=1, replica_groups=mesh['groups'=2,'ctx'=32,'rep'=4,'row'=2] {'ctx'}, dimensions={0} | all-to-all | bytes 8192 | tf_op jit(solution)/shard_map/all_to_all | solution.py:12
  68.8 0.9 tile.10
  69.7 4.9 %all-to-all-start.1 = ((bf16[4,32,16,128]{3,2,0,1:T(8,128)(2,1)}), bf16[4,32,16,128]{3,2,0,1:T(8,128)(2,1)S(1)}, u32[]{:S(2)}, u32[]{:S(2)}) async-start(bf16[4,32,16,128]{3,2,0,1:T(8,128)(2,1)} %tile.10), calls=%async_computation.1 | async-start | bytes 1048576 | tf_op jit(solution)/shard_map/all_to_all | solution.py:73
  74.7 1.4 select_reduce_fusion
  76.2 0.1 compare_reduce_fusion
  76.3 0.1 copy.51
  76.4 0.1 copy.49
  76.6 0.1 broadcast_in_dim.265
  76.8 0.1 broadcast_in_dim.272
  76.9 61.1 %all-to-all-done.1 = bf16[4,32,16,128]{3,2,0,1:T(8,128)(2,1)S(1)} async-done(((bf16[4,32,16,128]{3,2,0,1:T(8,128)(2,1)}), bf16[4,32,16,128]{3,2,0,1:T(8,128)(2,1)S(1)}, u32[]{:S(2)}, u32[]{:S(2)}) %all-to-all-start.1) | async-done | bytes 524320 | tf_op jit(solution)/shard_map/all_to_all | solution.py:73
  138.1 0.1 fusion.9
  138.2 0.1 fusion.11
  138.3 0.2 fusion.13
  138.5 0.3 fusion.22
  138.9 0.2 select_reduce_fusion.8
  139.1 0.4 copy-done.2
  139.5 0.4 fusion.48
  139.8 0.2 convolution_multiply_fusion.2
  140.1 0.2 convolution_multiply_fusion.4
  140.3 0.5 fusion.34
  140.9 0.4 fusion.44
  141.3 0.4 fusion.42
  141.6 0.7 fusion.36
  142.3 0.4 fusion.46
  142.8 0.1 max.136
  142.9 0.2 fusion.10
  143.1 0.2 fusion.12
  143.2 0.2 fusion.14
  143.4 0.3 fusion.18
  143.7 0.2 select_reduce_fusion.9
  143.9 0.4 fusion.56
  144.3 0.2 convolution_multiply_fusion.3
  144.5 0.2 convolution_multiply_fusion.5
  144.8 0.5 fusion.26
  145.3 0.4 fusion.52
  145.7 0.4 fusion.50
  146.1 0.7 fusion.28
  146.8 0.4 fusion.54
  147.3 0.1 max.134
  147.5 0.6 copy-done.3
  148.2 0.2 fusion.6
  148.4 0.2 fusion.4
  148.6 0.2 fusion
  148.9 0.2 fusion.2
  149.5 0.2 fusion.7
  149.8 0.2 fusion.5
  150.0 0.2 fusion.1
  150.2 0.2 fusion.3
  151.2 0.7 copy.58
  151.8 4.8 %all-to-all-start.4 = ((f32[1,4,32,16]{3,1,0,2:T(4,128)}), f32[1,4,32,16]{3,1,0,2:T(4,128)S(1)}, u32[]{:S(2)}, u32[]{:S(2)}) async-start(f32[1,4,32,16]{3,1,0,2:T(4,128)} %copy.58), calls=%async_computation.4 | async-start | bytes 131072 | tf_op jit(solution)/shard_map/all_to_all | solution.py:153
  156.9 0.7 copy.52
  157.7 22.7 %all-to-all-done.4 = f32[1,4,32,16]{3,1,0,2:T(4,128)S(1)} async-done(((f32[1,4,32,16]{3,1,0,2:T(4,128)}), f32[1,4,32,16]{3,1,0,2:T(4,128)S(1)}, u32[]{:S(2)}, u32[]{:S(2)}) %all-to-all-start.4) | async-done | bytes 8224 | tf_op jit(solution)/shard_map/all_to_all | solution.py:153
  180.3 4.8 %all-to-all-start.2 = ((f32[1,4,32,16]{3,1,0,2:T(4,128)}), f32[1,4,32,16]{3,1,0,2:T(4,128)S(1)}, u32[]{:S(2)}, u32[]{:S(2)}) async-start(f32[1,4,32,16]{3,1,0,2:T(4,128)} %copy.52), calls=%async_computation.2 | async-start | bytes 131072 | tf_op jit(solution)/shard_map/all_to_all | solution.py:152
  185.1 1.1 maximum_bitcast_fusion
  186.2 22.7 %all-to-all-done.2 = f32[1,4,32,16]{3,1,0,2:T(4,128)S(1)} async-done(((f32[1,4,32,16]{3,1,0,2:T(4,128)}), f32[1,4,32,16]{3,1,0,2:T(4,128)S(1)}, u32[]{:S(2)}, u32[]{:S(2)}) %all-to-all-start.2) | async-done | bytes 8224 | tf_op jit(solution)/shard_map/all_to_all | solution.py:152
  208.8 4.8 %all-to-all-start.3 = ((f32[1,4,32,16,128]{4,3,1,0,2:T(8,128)}), f32[1,4,32,16,128]{4,3,1,0,2:T(8,128)S(1)}, u32[]{:S(2)}, u32[]{:S(2)}) async-start(f32[1,4,32,16,128]{4,3,1,0,2:T(8,128)} %maximum_bitcast_fusion), calls=%async_computation.3 | async-start | bytes 2097152 | tf_op jit(solution)/shard_map/all_to_all | solution.py:154
  213.7 0.7 copy-done.8
  214.4 0.2 select_reduce_fusion.1
  214.6 0.1 fusion.122
  214.8 0.3 convolution_bitcast_fusion
  215.3 103.4 %all-to-all-done.3 = f32[1,4,32,16,128]{4,3,1,0,2:T(8,128)S(1)} async-done(((f32[1,4,32,16,128]{4,3,1,0,2:T(8,128)}), f32[1,4,32,16,128]{4,3,1,0,2:T(8,128)S(1)}, u32[]{:S(2)}, u32[]{:S(2)}) %all-to-all-start.3) | async-done | bytes 1048608 | tf_op jit(solution)/shard_map/all_to_all | solution.py:154
  318.6 0.3 fusion.17
  319.0 0.7 fusion.121
  (76 shorter events, 2.7 us)
Async XLA Ops:
  0.0 214.8 %copy-start = (bf16[4,1,2,128]{3,2,1,0:T(2,128)(2,1)S(1)}, bf16[4,1,2,128]{3,2,1,0:T(2,128)(2,1)}, u32[]{:S(2)}) copy-start(bf16[4,1,2,128]{3,2,1,0:T(2,128)(2,1)} %param.11) | copy-start | bytes 6148
  0.0 0.7 copy-start.6
  0.7 68.1 %copy-start.4 = (bf16[4,1,16,128]{3,2,1,0:T(8,128)(2,1)S(1)}, bf16[4,1,16,128]{3,2,1,0:T(8,128)(2,1)}, u32[]{:S(2)}) copy-start(bf16[4,1,16,128]{3,2,1,0:T(8,128)(2,1)} %param.9) | copy-start | bytes 49156
  69.7 5.0 %copy-start.5 = (s32[2,128]{1,0:T(2,128)S(1)}, s32[2,128]{1,0:T(2,128)}, u32[]{:S(2)}) copy-start(s32[2,128]{1,0:T(2,128)} %param.16) | copy-start | bytes 3076
  69.7 68.4 %all-to-all-start.1 = ((bf16[4,32,16,128]{3,2,0,1:T(8,128)(2,1)}), bf16[4,32,16,128]{3,2,0,1:T(8,128)(2,1)S(1)}, u32[]{:S(2)}, u32[]{:S(2)}) async-start(bf16[4,32,16,128]{3,2,0,1:T(8,128)(2,1)} %tile.10), calls=%async_computation.1 | async-start | bytes 1048576 | tf_op jit(solution)/shard_map/all_to_all | solution.py:73
  74.7 63.9 %copy-start.1 = (bf16[2,512,128]{2,1,0:T(8,128)(2,1)S(1)}, bf16[2,512,128]{2,1,0:T(8,128)(2,1)}, u32[]{:S(2)}) copy-start(bf16[2,512,128]{2,1,0:T(8,128)(2,1)} %param.12) | copy-start | bytes 786436
  76.8 61.2 %copy-start.7 = (bf16[2,4,128]{2,1,0:T(4,128)(2,1)S(1)}, bf16[2,4,128]{2,1,0:T(4,128)(2,1)}, u32[]{:S(2)}) copy-start(bf16[2,4,128]{2,1,0:T(4,128)(2,1)} %param.14) | copy-start | bytes 6148
  138.5 1.0 copy-start.2
  147.5 0.7 copy-start.3
  151.8 28.5 %all-to-all-start.4 = ((f32[1,4,32,16]{3,1,0,2:T(4,128)}), f32[1,4,32,16]{3,1,0,2:T(4,128)S(1)}, u32[]{:S(2)}, u32[]{:S(2)}) async-start(f32[1,4,32,16]{3,1,0,2:T(4,128)} %copy.58), calls=%async_computation.4 | async-start | bytes 131072 | tf_op jit(solution)/shard_map/all_to_all | solution.py:153
  180.3 28.5 %all-to-all-start.2 = ((f32[1,4,32,16]{3,1,0,2:T(4,128)}), f32[1,4,32,16]{3,1,0,2:T(4,128)S(1)}, u32[]{:S(2)}, u32[]{:S(2)}) async-start(f32[1,4,32,16]{3,1,0,2:T(4,128)} %copy.52), calls=%async_computation.2 | async-start | bytes 131072 | tf_op jit(solution)/shard_map/all_to_all | solution.py:152
  208.8 109.8 %all-to-all-start.3 = ((f32[1,4,32,16,128]{4,3,1,0,2:T(8,128)}), f32[1,4,32,16,128]{4,3,1,0,2:T(8,128)S(1)}, u32[]{:S(2)}, u32[]{:S(2)}) async-start(f32[1,4,32,16,128]{4,3,1,0,2:T(8,128)} %maximum_bitcast_fusion), calls=%async_computation.3 | async-start | bytes 2097152 | tf_op jit(solution)/shard_map/all_to_all | solution.py:154
  213.7 0.7 copy-start.8
